TPU v7x, 32 devices: a whole 2x2x4 slice. The times are simulated.
32 devices in a mesh: dp: 4 (over z), table: 8 (over y, x, core).
Axes of the slice: x: 2, y: 2, z: 4, core: 2. Of those that a mesh axis runs over, the one named last changes fastest.
Arguments:
- table: bfloat16 [4096, 256], P('table'), may hold values from -6 to 6
- weights: bfloat16 [2, 6, 256, 256], replicated, may hold values from -0.375 to 0.375
- fetch_rows: int32 [4, 8, 8, 32], P('dp', 'table'), may hold values from 0 to 511
- fetch_count: int32 [4, 8, 8], P('dp', 'table'), may hold values from 1 to 32, as said below
- first_self: int32 [4, 8, 256], P('dp', 'table'), may hold values from 0 to 255, as said below
- first_edges: int32 [4, 8, 5, 256, 4], P('dp', 'table'), may hold values from 0 to 255, as said below
- first_degree: int32 [4, 8, 5, 256], P('dp', 'table'), may hold values from 1 to 4
- second_self: int32 [4, 8, 128], P('dp', 'table'), may hold values from 0 to 255
- second_edges: int32 [4, 8, 5, 128, 4], P('dp', 'table'), may hold values from 0 to 255
- second_degree: int32 [4, 8, 5, 128], P('dp', 'table'), may hold values from 1 to 4
- cotangent: bfloat16 [4, 8, 128, 256], P('dp', 'table'), may hold values from -6 to 6
Outputs:
- node_out: bfloat16 [4, 8, 128, 256], P('dp', 'table')
- weight_grad: bfloat16 [2, 6, 256, 256], replicated
- table_grad: float32 [8, 512, 256], P('table', 'dp')
Inputs may be any that keep to these rules, and one draw needn't show every extreme that they name: Minibatch (i, j) uses the first fetch_count[i, j, k] slots for shard k; for each i one shard is given all 32 slots by every minibatch of that i, and every other count is at most 16. `fetch_rows`: slots past the count hold arbitrary row numbers. `first_self`: every entry is a live slot k * 32 + c with c < fetch_count of shard k. `first_edges`: every entry, used or not, is a live slot k * 32 + c with c < fetch_count of shard k.
All inputs are finite; a program needn't handle non-finite values.
Results may differ from a plain program's by a relative error of at most 0.0057.
Values may be sent and summed in bfloat16 or wider, within the bound.
A program may use at most 64 MiB of HBM per device.

v0:
```python
import jax
import jax.numpy as jnp
from jax import lax
from jax.sharding import PartitionSpec as P


def aggregate(features, edges, degrees):

    def aggregate_single(bundle):
        indices, degree = bundle
        within = lax.broadcasted_iota(jnp.int32, indices.shape, 1) < degree[:, None]
        picked = jnp.where(within[:, :, None], features[indices], jnp.zeros((), features.dtype))
        summed = jnp.sum(picked.astype(jnp.float32), axis=1)
        return (summed / degree[:, None].astype(jnp.float32)).astype(jnp.bfloat16)

    return lax.map(aggregate_single, (edges, degrees))


def spread_back(grads, edges, degrees, height):

    def spread_single(running, bundle):
        part_grad, indices, degree = bundle
        within = lax.broadcasted_iota(jnp.int32, indices.shape, 1) < degree[:, None]
        scaled = part_grad / degree[:, None].astype(part_grad.dtype)
        placed = jnp.where(within[:, :, None], scaled[:, None, :], jnp.zeros((), part_grad.dtype))
        return (running.at[indices.reshape(-1)].add(placed.reshape(-1, part_grad.shape[-1])), None)

    initial = jnp.zeros((height, grads.shape[-1]), grads.dtype)
    result, ignored = lax.scan(spread_single, initial, (grads, edges, degrees))
    return result


def relation_sum(agg, layer_weights):
    return jnp.einsum("rbd,rde->be", agg, layer_weights, preferred_element_type=jnp.float32)


def silu_slope(preact):
    logistic = jax.nn.sigmoid(preact)
    return logistic * (1.0 + preact * (1.0 - logistic))


def weight_terms(own_rows, agg, grad):
    own_term = lax.dot_general(
        own_rows, grad, (((0,), (0,)), ((), ())), preferred_element_type=jnp.float32
    )
    rel_terms = jnp.einsum("rbd,be->rde", agg, grad, preferred_element_type=jnp.float32)
    return jnp.concatenate([own_term[None], rel_terms], axis=0)


def input_terms(grad, layer_weights):
    own_back = lax.dot_general(
        grad, layer_weights[0], (((1,), (1,)), ((), ())), preferred_element_type=jnp.float32
    )
    rel_back = jnp.einsum(
        "be,rde->rbd", grad, layer_weights[1:], preferred_element_type=jnp.float32
    )
    return (own_back, rel_back)


def body(
    table,
    weights,
    fetch_rows,
    fetch_count,
    first_self,
    first_edges,
    first_degree,
    second_self,
    second_edges,
    second_degree,
    cotangent,
):
    wanted = fetch_rows[0, 0]
    live_count = fetch_count[0, 0]
    first_self = first_self[0, 0]
    first_edges = first_edges[0, 0]
    first_degree = first_degree[0, 0]
    second_self = second_self[0, 0]
    second_edges = second_edges[0, 0]
    second_degree = second_degree[0, 0]
    cot_rows = cotangent[0, 0]
    shards = wanted.shape[0]
    width = wanted.shape[1]
    feature = table.shape[1]
    asked = lax.all_to_all(wanted, "table", split_axis=0, concat_axis=0, tiled=True)
    found = table[asked]
    fetched, asked = (
        lax.all_to_all(found, "table", split_axis=0, concat_axis=0, tiled=True),
        asked,
    )
    living = lax.broadcasted_iota(jnp.int32, wanted.shape, 1) < live_count[:, None]
    inputs = jnp.where(living[:, :, None], fetched, jnp.zeros((), fetched.dtype)).reshape(
        -1, feature
    )
    first_agg = aggregate(inputs, first_edges, first_degree)
    first_own = inputs[first_self]
    first_pre = jnp.dot(
        first_own, weights[0, 0], preferred_element_type=jnp.float32
    ) + relation_sum(first_agg, weights[0, 1:])
    hidden = jax.nn.silu(first_pre).astype(jnp.bfloat16)
    second_agg = aggregate(hidden, second_edges, second_degree)
    second_own = hidden[second_self]
    output = jnp.dot(second_own, weights[1, 0], preferred_element_type=jnp.float32) + relation_sum(
        second_agg, weights[1, 1:]
    )
    node_out = output.astype(jnp.bfloat16)
    grad_top = weight_terms(second_own, second_agg, cot_rows)
    own_back, rel_back = input_terms(cot_rows, weights[1])
    grad_hidden = (
        jnp.zeros((hidden.shape[0], hidden.shape[1]), jnp.float32).at[second_self].add(own_back)
    )
    grad_hidden = grad_hidden + spread_back(rel_back, second_edges, second_degree, hidden.shape[0])
    grad_pre = (grad_hidden * silu_slope(first_pre)).astype(jnp.bfloat16)
    grad_bottom = weight_terms(first_own, first_agg, grad_pre)
    own_back, rel_back = input_terms(grad_pre, weights[0])
    grad_slots = (
        jnp.zeros((inputs.shape[0], inputs.shape[1]), jnp.float32).at[first_self].add(own_back)
    )
    grad_slots = grad_slots + spread_back(rel_back, first_edges, first_degree, inputs.shape[0])
    grad_slots = jnp.where(living.reshape(-1)[:, None], grad_slots, jnp.zeros((), grad_slots.dtype))
    grad_bottom, grad_top = lax.psum((grad_bottom, grad_top), ("dp", "table"))
    seeds = cot_rows.shape[0] * lax.axis_size("dp") * lax.axis_size("table")
    weight_grad = (jnp.stack([grad_bottom, grad_top]) / jnp.sqrt(jnp.float32(seeds))).astype(
        jnp.bfloat16
    )
    slot_grads = grad_slots.reshape(shards, width, feature)
    returned = lax.all_to_all(slot_grads, "table", split_axis=0, concat_axis=0, tiled=True)
    dense = (
        jnp.zeros((table.shape[0], feature), jnp.float32)
        .at[asked.reshape(-1)]
        .add(returned.reshape(-1, feature))
    )
    table_part = lax.psum_scatter(dense, "dp", scatter_dimension=0, tiled=True)
    return (node_out[None, None], weight_grad, table_part[None])


def solution(mesh):
    return jax.shard_map(
        body,
        mesh=mesh,
        in_specs=(
            P("table", None),
            P(),
            P("dp", "table", None, None),
            P("dp", "table", None),
            P("dp", "table", None),
            P("dp", "table", None, None, None),
            P("dp", "table", None, None),
            P("dp", "table", None),
            P("dp", "table", None, None, None),
            P("dp", "table", None, None),
            P("dp", "table", None, None),
        ),
        out_specs=(P("dp", "table", None, None), P(), P("table", "dp", None)),
        check_vma=False,
    )
```

profile of v0, /device:TPU:0, one launch (start us, length us, event | category | flops | bytes accessed | tf_op | source)
XLA Modules:
  0.0 262.6 jit_solution(11616878313008494928)
XLA Ops:
  8.0 5.3 %all-to-all-start = ((s32[8,1,32]{2,1,0:T(1,128)}), s32[8,1,32]{2,1,0:T(1,128)S(1)}, u32[]{:S(2)}, u32[]{:S(2)}) async-start(s32[8,1,32]{2,1,0:T(1,128)} %bitcast.161), calls=%async_computation | async-start | bytes 8192 | tf_op jit(solution)/shard_map/all_to_all | solution.py:85
  16.2 22.4 %while.42 = (s32[]{:T(128)}, f32[256,256]{1,0:T(8,128)S(1)}, s32[5,128,4]{2,1,0:T(8,128)S(1)}, s32[5,128]{1,0:T(8,128)S(1)}, f32[5,128,256]{1,2,0:T(8,128)S(1)}, /*index=5*/s32[]{:T(128)}, f32[]{:T(128)}) while((s32[]{:T(128)}, f32[256,256]{1,0:T(8,128)S(1)}, s32[5,128,4]{2,1,0:T(8,128)S(1)}, s32[5,128]{1,0:T(8,128)S(1)}, ...), condition=%wide.region_8.9_spmd, body=%wide.region_6.8_spmd.sunk | while | flops 297090 | bytes 3293797 | solution.py:29
  17.1 3.6 %scatter_custom_fusion.13 = f32[256,256]{1,0:T(8,128)S(1)} fusion(f32[256,256]{1,0:T(8,128)S(1)} %get-tuple-element.320, s32[512]{0:T(512)S(1)} %bitcast.155, f32[512,256]{1,0:T(8,128)S(1)} %broadcast_in_dim.194, f32[]{:T(128)} %constant.66.clone.1..sunk, pred[512]{0:T(512)(128)(4,1)S(1)} %lt.237), kind=kCustom, calls=%fused_computation.27.clone.1 | custom fusion | flops 262144 | bytes 786948 | tf_op jit(solution)/shard_map/while/body/eval_jaxpr/scatter-add | solution.py:26
  21.6 3.6 %scatter_custom_fusion.13 = f32[256,256]{1,0:T(8,128)S(1)} fusion(f32[256,256]{1,0:T(8,128)S(1)} %get-tuple-element.320, s32[512]{0:T(512)S(1)} %bitcast.155, f32[512,256]{1,0:T(8,128)S(1)} %broadcast_in_dim.194, f32[]{:T(128)} %constant.66.clone.1..sunk, pred[512]{0:T(512)(128)(4,1)S(1)} %lt.237), kind=kCustom, calls=%fused_computation.27.clone.1 | custom fusion | flops 262144 | bytes 786948 | tf_op jit(solution)/shard_map/while/body/eval_jaxpr/scatter-add | solution.py:26
  26.1 3.6 %scatter_custom_fusion.13 = f32[256,256]{1,0:T(8,128)S(1)} fusion(f32[256,256]{1,0:T(8,128)S(1)} %get-tuple-element.320, s32[512]{0:T(512)S(1)} %bitcast.155, f32[512,256]{1,0:T(8,128)S(1)} %broadcast_in_dim.194, f32[]{:T(128)} %constant.66.clone.1..sunk, pred[512]{0:T(512)(128)(4,1)S(1)} %lt.237), kind=kCustom, calls=%fused_computation.27.clone.1 | custom fusion | flops 262144 | bytes 786948 | tf_op jit(solution)/shard_map/while/body/eval_jaxpr/scatter-add | solution.py:26
  30.6 3.6 %scatter_custom_fusion.13 = f32[256,256]{1,0:T(8,128)S(1)} fusion(f32[256,256]{1,0:T(8,128)S(1)} %get-tuple-element.320, s32[512]{0:T(512)S(1)} %bitcast.155, f32[512,256]{1,0:T(8,128)S(1)} %broadcast_in_dim.194, f32[]{:T(128)} %constant.66.clone.1..sunk, pred[512]{0:T(512)(128)(4,1)S(1)} %lt.237), kind=kCustom, calls=%fused_computation.27.clone.1 | custom fusion | flops 262144 | bytes 786948 | tf_op jit(solution)/shard_map/while/body/eval_jaxpr/scatter-add | solution.py:26
  35.0 3.6 %scatter_custom_fusion.13 = f32[256,256]{1,0:T(8,128)S(1)} fusion(f32[256,256]{1,0:T(8,128)S(1)} %get-tuple-element.320, s32[512]{0:T(512)S(1)} %bitcast.155, f32[512,256]{1,0:T(8,128)S(1)} %broadcast_in_dim.194, f32[]{:T(128)} %constant.66.clone.1..sunk, pred[512]{0:T(512)(128)(4,1)S(1)} %lt.237), kind=kCustom, calls=%fused_computation.27.clone.1 | custom fusion | flops 262144 | bytes 786948 | tf_op jit(solution)/shard_map/while/body/eval_jaxpr/scatter-add | solution.py:26
  40.6 4.2 %all-to-all-start.1 = ((bf16[8,32,256]{2,1,0:T(8,128)(2,1)}), bf16[8,32,256]{2,1,0:T(8,128)(2,1)S(1)}, u32[]{:S(2)}, u32[]{:S(2)}) async-start(bf16[8,32,256]{2,1,0:T(8,128)(2,1)} %bitcast.15), calls=%async_computation.1 | async-start | bytes 262144 | tf_op jit(solution)/shard_map/all_to_all | solution.py:88
  47.4 2.9 %all-to-all-done.1 = bf16[8,32,256]{2,1,0:T(8,128)(2,1)S(1)} async-done(((bf16[8,32,256]{2,1,0:T(8,128)(2,1)}), bf16[8,32,256]{2,1,0:T(8,128)(2,1)S(1)}, u32[]{:S(2)}, u32[]{:S(2)}) %all-to-all-start.1) | async-done | bytes 131104 | tf_op jit(solution)/shard_map/all_to_all | solution.py:88
  50.5 33.3 %while.40 = (s32[]{:T(128)}, bf16[5,256,256]{2,1,0:T(8,128)(2,1)}, s32[5,256]{1,0:T(8,128)S(1)}, s32[5,256,4]{2,1,0:T(8,128)S(1)}, bf16[256,256]{1,0:T(8,128)(2,1)S(1)}, /*index=5*/s32[]{:T(128)}) while((s32[]{:T(128)}, bf16[5,256,256]{2,1,0:T(8,128)(2,1)}, s32[5,256]{1,0:T(8,128)S(1)}, s32[5,256,4]{2,1,0:T(8,128)S(1)}, ...), condition=%wide.region_2.3_spmd, body=%wide.region_0.2_spmd.sunk | while | flops 857346 | bytes 3313753 | solution.py:16
  50.6 3.9 %gather_fusion = bf16[1024,256]{1,0:T(8,128)(2,1)S(1)} fusion(bf16[256,256]{1,0:T(8,128)(2,1)S(1)} %get-tuple-element.349, s32[1024]{0:T(1024)S(1)} %broadcast_clamp_fusion.2), kind=kCustom, calls=%fused_computation.clone.1 | custom fusion | bytes 1052672 | tf_op jit(solution)/shard_map/while/body/eval_jaxpr/gather | solution.py:12
  57.3 3.9 %gather_fusion = bf16[1024,256]{1,0:T(8,128)(2,1)S(1)} fusion(bf16[256,256]{1,0:T(8,128)(2,1)S(1)} %get-tuple-element.349, s32[1024]{0:T(1024)S(1)} %broadcast_clamp_fusion.2), kind=kCustom, calls=%fused_computation.clone.1 | custom fusion | bytes 1052672 | tf_op jit(solution)/shard_map/while/body/eval_jaxpr/gather | solution.py:12
  63.9 3.9 %gather_fusion = bf16[1024,256]{1,0:T(8,128)(2,1)S(1)} fusion(bf16[256,256]{1,0:T(8,128)(2,1)S(1)} %get-tuple-element.349, s32[1024]{0:T(1024)S(1)} %broadcast_clamp_fusion.2), kind=kCustom, calls=%fused_computation.clone.1 | custom fusion | bytes 1052672 | tf_op jit(solution)/shard_map/while/body/eval_jaxpr/gather | solution.py:12
  70.6 3.9 %gather_fusion = bf16[1024,256]{1,0:T(8,128)(2,1)S(1)} fusion(bf16[256,256]{1,0:T(8,128)(2,1)S(1)} %get-tuple-element.349, s32[1024]{0:T(1024)S(1)} %broadcast_clamp_fusion.2), kind=kCustom, calls=%fused_computation.clone.1 | custom fusion | bytes 1052672 | tf_op jit(solution)/shard_map/while/body/eval_jaxpr/gather | solution.py:12
  77.2 3.9 %gather_fusion = bf16[1024,256]{1,0:T(8,128)(2,1)S(1)} fusion(bf16[256,256]{1,0:T(8,128)(2,1)S(1)} %get-tuple-element.349, s32[1024]{0:T(1024)S(1)} %broadcast_clamp_fusion.2), kind=kCustom, calls=%fused_computation.clone.1 | custom fusion | bytes 1052672 | tf_op jit(solution)/shard_map/while/body/eval_jaxpr/gather | solution.py:12
  89.1 2.6 convolution_bitcast_fusion
  91.7 17.2 %while.41 = (s32[]{:T(128)}, bf16[5,128,256]{2,1,0:T(8,128)(2,1)}, s32[5,128]{1,0:T(8,128)S(1)}, s32[5,128,4]{2,1,0:T(8,128)S(1)}, bf16[256,256]{1,0:T(8,128)(2,1)S(1)}, /*index=5*/s32[]{:T(128)}) while((s32[]{:T(128)}, bf16[5,128,256]{2,1,0:T(8,128)(2,1)}, s32[5,128]{1,0:T(8,128)S(1)}, s32[5,128,4]{2,1,0:T(8,128)S(1)}, ...), condition=%wide.region_5.6_spmd, body=%wide.region_3.5_spmd.sunk | while | flops 429186 | bytes 1658457 | solution.py:16
  91.8 2.0 gather_fusion.1
  95.2 2.0 gather_fusion.1
  98.7 2.0 gather_fusion.1
  113.2 44.2 %while.43 = (s32[]{:T(128)}, f32[256,256]{1,0:T(8,128)S(1)}, s32[5,256,4]{2,1,0:T(8,128)S(1)}, s32[5,256]{1,0:T(8,128)S(1)}, f32[5,256,256]{2,1,0:T(8,128)}, /*index=5*/s32[]{:T(128)}, f32[]{:T(128)}) while((s32[]{:T(128)}, f32[256,256]{1,0:T(8,128)S(1)}, s32[5,256,4]{2,1,0:T(8,128)S(1)}, s32[5,256]{1,0:T(8,128)S(1)}, ...), condition=%wide.region_14.15_spmd, body=%wide.region_12.14_spmd.sunk | while | flops 594178 | bytes 5277797 | solution.py:29
  115.3 6.8 %scatter_custom_fusion.15 = f32[256,256]{1,0:T(8,128)S(1)} fusion(f32[256,256]{1,0:T(8,128)S(1)} %get-tuple-element.377, s32[1024]{0:T(1024)S(1)} %bitcast.154, f32[1024,256]{1,0:T(8,128)S(1)} %broadcast_in_dim.198, f32[]{:T(128)} %constant.66.clone.1..sunk.1, pred[1024]{0:T(1024)(128)(4,1)S(1)} %lt.241), kind=kCustom, calls=%fused_computation.38.clone.1 | custom fusion | flops 524288 | bytes 1311748 | tf_op jit(solution)/shard_map/while/body/eval_jaxpr/scatter-add | solution.py:26
  124.1 6.8 %scatter_custom_fusion.15 = f32[256,256]{1,0:T(8,128)S(1)} fusion(f32[256,256]{1,0:T(8,128)S(1)} %get-tuple-element.377, s32[1024]{0:T(1024)S(1)} %bitcast.154, f32[1024,256]{1,0:T(8,128)S(1)} %broadcast_in_dim.198, f32[]{:T(128)} %constant.66.clone.1..sunk.1, pred[1024]{0:T(1024)(128)(4,1)S(1)} %lt.241), kind=kCustom, calls=%fused_computation.38.clone.1 | custom fusion | flops 524288 | bytes 1311748 | tf_op jit(solution)/shard_map/while/body/eval_jaxpr/scatter-add | solution.py:26
  133.0 6.8 %scatter_custom_fusion.15 = f32[256,256]{1,0:T(8,128)S(1)} fusion(f32[256,256]{1,0:T(8,128)S(1)} %get-tuple-element.377, s32[1024]{0:T(1024)S(1)} %bitcast.154, f32[1024,256]{1,0:T(8,128)S(1)} %broadcast_in_dim.198, f32[]{:T(128)} %constant.66.clone.1..sunk.1, pred[1024]{0:T(1024)(128)(4,1)S(1)} %lt.241), kind=kCustom, calls=%fused_computation.38.clone.1 | custom fusion | flops 524288 | bytes 1311748 | tf_op jit(solution)/shard_map/while/body/eval_jaxpr/scatter-add | solution.py:26
  141.8 6.8 %scatter_custom_fusion.15 = f32[256,256]{1,0:T(8,128)S(1)} fusion(f32[256,256]{1,0:T(8,128)S(1)} %get-tuple-element.377, s32[1024]{0:T(1024)S(1)} %bitcast.154, f32[1024,256]{1,0:T(8,128)S(1)} %broadcast_in_dim.198, f32[]{:T(128)} %constant.66.clone.1..sunk.1, pred[1024]{0:T(1024)(128)(4,1)S(1)} %lt.241), kind=kCustom, calls=%fused_computation.38.clone.1 | custom fusion | flops 524288 | bytes 1311748 | tf_op jit(solution)/shard_map/while/body/eval_jaxpr/scatter-add | solution.py:26
  150.7 6.8 %scatter_custom_fusion.15 = f32[256,256]{1,0:T(8,128)S(1)} fusion(f32[256,256]{1,0:T(8,128)S(1)} %get-tuple-element.377, s32[1024]{0:T(1024)S(1)} %bitcast.154, f32[1024,256]{1,0:T(8,128)S(1)} %broadcast_in_dim.198, f32[]{:T(128)} %constant.66.clone.1..sunk.1, pred[1024]{0:T(1024)(128)(4,1)S(1)} %lt.241), kind=kCustom, calls=%fused_computation.38.clone.1 | custom fusion | flops 524288 | bytes 1311748 | tf_op jit(solution)/shard_map/while/body/eval_jaxpr/scatter-add | solution.py:26
  158.6 2.1 scatter_fusion.1
  161.6 3.4 %all-to-all-start.2 = ((f32[8,32,256]{2,1,0:T(8,128)}), f32[8,32,256]{2,1,0:T(8,128)S(1)}, u32[]{:S(2)}, u32[]{:S(2)}) async-start(f32[8,32,256]{2,1,0:T(8,128)} %bitcast.41), calls=%async_computation.2 | async-start | bytes 524288 | tf_op jit(solution)/shard_map/all_to_all | solution.py:127
  166.3 6.1 %all-to-all-done.2 = f32[8,32,256]{2,1,0:T(8,128)S(1)} async-done(((f32[8,32,256]{2,1,0:T(8,128)}), f32[8,32,256]{2,1,0:T(8,128)S(1)}, u32[]{:S(2)}, u32[]{:S(2)}) %all-to-all-start.2) | async-done | bytes 262176 | tf_op jit(solution)/shard_map/all_to_all | solution.py:127
  172.3 2.7 %scatter_custom_fusion.4 = f32[512,256]{1,0:T(8,128)} fusion(s32[256]{0:T(256)S(1)} %bitcast.162, f32[256,256]{1,0:T(8,128)S(1)} %bitcast.149, f32[]{:T(128)} %constant.66.clone.1), kind=kCustom, calls=%fused_computation.69 | custom fusion | flops 65536 | bytes 524292 | tf_op jit(solution)/shard_map/scatter-add | solution.py:131
  176.2 75.6 %all-reduce.3.cloned.1.call-done = (f32[1,6,256,256]{3,2,1,0:T(8,128)}, f32[1,6,256,256]{3,2,1,0:T(8,128)}) async-done(((f32[1,6,256,256]{3,2,1,0:T(8,128)}, f32[1,6,256,256]{3,2,1,0:T(8,128)}), (f32[1,6,256,256]{3,2,1,0:T(8,128)}, f32[1,6,256,256]{3,2,1,0:T(8,128)})) %all-reduce.3.cloned.1.call-update) | async-done | bytes 3145744 | tf_op jit(solution)/shard_map/psum | solution.py:121
  251.8 3.4 %fusion.14 = bf16[2,6,256,256]{3,2,1,0:T(8,128)(2,1)} fusion(f32[1,6,256,256]{3,2,1,0:T(8,128)} %get-tuple-element.170, f32[1,6,256,256]{3,2,1,0:T(8,128)} %get-tuple-element.171), kind=kLoop, calls=%fused_computation.48 | loop fusion | flops 2359296 | bytes 4718592 | tf_op jit(solution)/shard_map/convert_element_type | solution.py:123
  (265 shorter events, 59.8 us)
Async XLA Ops:
  8.0 30.8 %copy-start = (bf16[512,256]{1,0:T(8,128)(2,1)S(1)}, bf16[512,256]{1,0:T(8,128)(2,1)}, u32[]{:S(2)}) copy-start(bf16[512,256]{1,0:T(8,128)(2,1)} %param.19) | copy-start | bytes 786436
  8.0 7.9 %copy-start.9 = (s32[1,1,5,128]{3,1,2,0:T(1,128)S(1)}, s32[1,1,5,128]{3,1,2,0:T(1,128)}, u32[]{:S(2)}) copy-start(s32[1,1,5,128]{3,1,2,0:T(1,128)} %param.28) | copy-start | bytes 7684
  8.0 7.9 %copy-start.7 = (s32[1,1,5,128,4]{3,4,2,1,0:T(4,128)S(1)}, s32[1,1,5,128,4]{3,4,2,1,0:T(4,128)}, u32[]{:S(2)}) copy-start(s32[1,1,5,128,4]{3,4,2,1,0:T(4,128)} %param.27) | copy-start | bytes 30724
  8.0 30.7 %all-to-all-start = ((s32[8,1,32]{2,1,0:T(1,128)}), s32[8,1,32]{2,1,0:T(1,128)S(1)}, u32[]{:S(2)}, u32[]{:S(2)}) async-start(s32[8,1,32]{2,1,0:T(1,128)} %bitcast.161), calls=%async_computation | async-start | bytes 8192 | tf_op jit(solution)/shard_map/all_to_all | solution.py:85
  16.2 22.5 %copy-start.12 = (s32[1,1,8]{2,1,0:T(1,128)S(1)}, s32[1,1,8]{2,1,0:T(1,128)}, u32[]{:S(2)}) copy-start(s32[1,1,8]{2,1,0:T(1,128)} %param.22) | copy-start | bytes 100
  16.2 22.5 %copy-start.10 = (s32[1,1,256]{2,1,0:T(1,128)S(1)}, s32[1,1,256]{2,1,0:T(1,128)}, u32[]{:S(2)}) copy-start(s32[1,1,256]{2,1,0:T(1,128)} %param.23) | copy-start | bytes 3076
  16.2 22.5 %copy-start.13 = (s32[1,1,128]{2,1,0:T(1,128)S(1)}, s32[1,1,128]{2,1,0:T(1,128)}, u32[]{:S(2)}) copy-start(s32[1,1,128]{2,1,0:T(1,128)} %param.26) | copy-start | bytes 1540
  16.2 28.7 %copy-start.8 = (s32[1,1,5,256]{3,1,2,0:T(1,128)S(1)}, s32[1,1,5,256]{3,1,2,0:T(1,128)}, u32[]{:S(2)}) copy-start(s32[1,1,5,256]{3,1,2,0:T(1,128)} %param.25) | copy-start | bytes 15364
  16.2 28.7 %copy-start.6 = (s32[1,1,5,256,4]{3,4,2,1,0:T(4,128)S(1)}, s32[1,1,5,256,4]{3,4,2,1,0:T(4,128)}, u32[]{:S(2)}) copy-start(s32[1,1,5,256,4]{3,4,2,1,0:T(4,128)} %param.24) | copy-start | bytes 61444
  40.6 9.7 %all-to-all-start.1 = ((bf16[8,32,256]{2,1,0:T(8,128)(2,1)}), bf16[8,32,256]{2,1,0:T(8,128)(2,1)S(1)}, u32[]{:S(2)}, u32[]{:S(2)}) async-start(bf16[8,32,256]{2,1,0:T(8,128)(2,1)} %bitcast.15), calls=%async_computation.1 | async-start | bytes 262144 | tf_op jit(solution)/shard_map/all_to_all | solution.py:88
  44.8 206.9 %all-reduce.3.cloned.1.call-start = ((), (), s32[]{:S(2)}) async-start(), calls=%async_computation.5 | async-start | bytes 6291456 | tf_op jit(solution)/shard_map/psum | solution.py:121
  86.5 1.3 copy-start.4
  91.7 18.0 %copy-start.3 = (bf16[1,1,128,256]{3,2,1,0:T(8,128)(2,1)S(1)}, bf16[1,1,128,256]{3,2,1,0:T(8,128)(2,1)}, u32[]{:S(2)}) copy-start(bf16[1,1,128,256]{3,2,1,0:T(8,128)(2,1)} %param.29) | copy-start | bytes 196612
  108.9 2.4 copy-start.2
  158.6 2.1 copy-start.11
  160.7 14.4 %copy-start.1 = (bf16[2,6,256,256]{3,2,1,0:T(8,128)(2,1)S(1)}, bf16[2,6,256,256]{3,2,1,0:T(8,128)(2,1)}, u32[]{:S(2)}) copy-start(bf16[2,6,256,256]{3,2,1,0:T(8,128)(2,1)} %param.20) | copy-start | bytes 4718596
  160.7 14.4 %copy-start.5 = (bf16[5,128,256]{2,1,0:T(8,128)(2,1)S(1)}, bf16[5,128,256]{2,1,0:T(8,128)(2,1)}, u32[]{:S(2)}) copy-start(bf16[5,128,256]{2,1,0:T(8,128)(2,1)} %get-tuple-element.112) | copy-start | bytes 983044
  161.6 10.8 %all-to-all-start.2 = ((f32[8,32,256]{2,1,0:T(8,128)}), f32[8,32,256]{2,1,0:T(8,128)S(1)}, u32[]{:S(2)}, u32[]{:S(2)}) async-start(f32[8,32,256]{2,1,0:T(8,128)} %bitcast.41), calls=%async_computation.2 | async-start | bytes 524288 | tf_op jit(solution)/shard_map/all_to_all | solution.py:127
  165.0 90.2 %reduce-scatter.2.cloned.1.call-start = ((), (), s32[]{:S(2)}) async-start(), calls=%async_computation.4 | async-start | bytes 655360 | tf_op jit(solution)/shard_map/reduce_scatter | solution.py:133
Sparse Core Ops, SparseCore 0:
  113.3 138.4 all-reduce.2
Sparse Core Ops, SparseCore 1:
  175.2 21.4 reduce-scatter.1
where the time goes:
time: 263 us
  other arithmetic  90.3 us (34%)
  waiting for transfers between devices  84.6 us (32%)
  local copies, waits for them, and re-layouts  44.5 us (17%)
  between operations  15.9 us (6%)
  starting transfers between devices  13 us (5%)
  matrix products  13 us (5%)
    psum x1, waiting for transfers between devices, body(): grad_bottom, grad_top = lax.psum((grad_bottom, grad_top), ('dp', 'table'))  75.6 us
    scatter-add x10, other arithmetic, spread_single(): running.at[indices.reshape(-1)].add(placed.reshape(-1, part_grad.shape[-1]))  51.7 us
    gather x20, local copies, waits for them, and re-layouts, aggregate_single(): features[indices]  30.4 us
    reduce_sum x10, other arithmetic, aggregate_single(): summed = jnp.sum(picked.astype(jnp.float32), axis=1)  9.69 us
    dynamic_update_slice x10, other arithmetic, aggregate(): return lax.map(aggregate_single, (edges, degrees))  7.46 us
    all_to_all x1, waiting for transfers between devices, body(): lax.all_to_all(slot_grads, 'table', split_axis=0, concat_axis=0, tiled=True)  6.05 us
    div x10, other arithmetic, spread_single(): scaled = part_grad / degree[:, None].astype(part_grad.dtype)  5.76 us
    all_to_all x1, starting transfers between devices, body(): lax.all_to_all(wanted, 'table', split_axis=0, concat_axis=0, tiled=True)  5.34 us
  transfers between devices with their start and end apart: 5, of which 3 were waited for; matrix products, arithmetic and copies ran while one was open for 32% of the time, Pallas kernels for 0%

commit v1 on v0

v1 whole, which is shorter than its diff:
```python
import functools
import math

import jax
import jax.numpy as jnp
from jax import lax
from jax.experimental import pallas as pl
from jax.experimental.pallas import tpu as pltpu
from jax.sharding import PartitionSpec as P

MESH = pl.DeviceIdType.MESH
VMEM = pltpu.VMEM
F32 = jnp.float32
BF16 = jnp.bfloat16


def dot(a, b, da, db):
    return lax.dot_general(a, b, (((da,), (db,)), ((), ())), preferred_element_type=F32)


def peer_on(axis, index):
    if axis == "dp":
        return (index, lax.axis_index("table"))
    return (lax.axis_index("dp"), index)


def greet(axes_sizes):
    barrier = pltpu.get_barrier_semaphore()
    total = 0
    for axis, size in axes_sizes:
        me = lax.axis_index(axis)
        for step in range(1, size):
            pl.semaphore_signal(
                barrier,
                inc=1,
                device_id=peer_on(axis, lax.rem(me + step, size)),
                device_id_type=MESH,
            )
            total += 1
    pl.semaphore_wait(barrier, total)


def pick_rows(row_numbers, height):
    shape = (height, row_numbers.shape[1])
    match = lax.broadcasted_iota(jnp.int32, shape, 0) == row_numbers
    return jnp.where(match, F32(1), F32(0)).astype(BF16)


def fetch_kernel(
    n_table, table, wanted, fetched, asked_row, asked_all, found, ssem, rsem, ssem2, rsem2
):
    me = lax.axis_index("table")
    greet((("table", n_table),))
    sends = []
    for step in range(1, n_table):
        copy = pltpu.make_async_remote_copy(
            src_ref=wanted,
            dst_ref=asked_all.at[me],
            send_sem=ssem.at[step],
            recv_sem=rsem.at[step],
            device_id=peer_on("table", lax.rem(me + step, n_table)),
            device_id_type=MESH,
        )
        copy.start()
        sends.append(copy)
    asked_all[me] = wanted[...]
    for copy in sends:
        copy.wait_recv()
    row = jnp.concatenate([asked_all[j, pl.ds(me, 1), :] for j in range(n_table)], axis=1)
    asked_row[...] = row
    selector = pick_rows(row, table.shape[0])
    found[...] = dot(selector, table[...], 0, 0).astype(BF16).reshape(found.shape)
    replies = []
    for step in range(1, n_table):
        peer = lax.rem(me + step, n_table)
        copy = pltpu.make_async_remote_copy(
            src_ref=found.at[peer],
            dst_ref=fetched.at[me],
            send_sem=ssem2.at[step],
            recv_sem=rsem2.at[step],
            device_id=peer_on("table", peer),
            device_id_type=MESH,
        )
        copy.start()
        replies.append(copy)
    fetched[me] = found[me]
    for copy in sends:
        copy.wait_send()
    for copy in replies:
        copy.wait()


def step_kernel(
    counts,
    fetched,
    weights,
    self1,
    edges1,
    degree1,
    self2,
    edges2,
    degree2,
    cot,
    node_out,
    grads,
    slot_grads,
    c1,
    c2,
    x1t,
    x2t,
    back1,
    back2,
):
    relations, fan, width1 = edges1.shape
    width2 = edges2.shape[2]
    shards, cap, feature = fetched.shape
    slots = shards * cap
    terms = relations + 1
    common = math.lcm(*range(1, fan + 1))
    inverse = F32(1.0 / common)

    live = []
    slot_pos = lax.broadcasted_iota(jnp.int32, (cap, feature), 0)
    for k in range(shards):
        live.append(slot_pos < counts[k])
    inputs = jnp.concatenate(
        [jnp.where(live[k], fetched[k].astype(F32), F32(0)) for k in range(shards)], axis=0
    ).astype(BF16)

    def fill(selector, own, edges, degree, height, width):
        spot = lax.broadcasted_iota(jnp.int32, (height, width), 0)
        selector[:, :width] = jnp.where(spot == own[...], F32(common), F32(0)).astype(BF16)
        for r in range(relations):
            deg = degree[r]
            share = F32(common) / deg.astype(F32)
            share = jnp.floor(share + F32(0.5))
            total = jnp.zeros((height, width), F32)
            for f in range(fan):
                where = jnp.where(deg > f, edges[r, f : f + 1, :], -1)
                total = total + jnp.where(spot == where, share, F32(0))
            selector[:, (r + 1) * width : (r + 2) * width] = total.astype(BF16)

    fill(c1, self1, edges1, degree1, slots, width1)
    fill(c2, self2, edges2, degree2, width1, width2)

    x1t[...] = (dot(inputs, c1[...], 0, 0) * inverse).astype(BF16)
    pre = jnp.zeros((width1, feature), F32)
    for r in range(terms):
        pre = pre + dot(x1t[:, r * width1 : (r + 1) * width1], weights[0, r], 0, 0)
    s = 1.0 / (1.0 + jnp.exp(-pre))
    hidden = (pre * s).astype(BF16)
    slope = s * (1.0 + pre * (1.0 - s))

    x2t[...] = (dot(hidden, c2[...], 0, 0) * inverse).astype(BF16)
    cot_rows = cot[...]
    out = jnp.zeros((width2, feature), F32)
    for r in range(terms):
        part = x2t[:, r * width2 : (r + 1) * width2]
        out = out + dot(part, weights[1, r], 0, 0)
        grads[1, r] = dot(part, cot_rows, 1, 0).astype(BF16)
        back2[r * width2 : (r + 1) * width2, :] = dot(cot_rows, weights[1, r], 1, 1).astype(BF16)
    node_out[...] = out.astype(BF16)

    grad_hidden = dot(c2[...], back2[...], 1, 0) * inverse
    grad_pre = (grad_hidden * slope).astype(BF16)
    for r in range(terms):
        part = x1t[:, r * width1 : (r + 1) * width1]
        grads[0, r] = dot(part, grad_pre, 1, 0).astype(BF16)
        back1[r * width1 : (r + 1) * width1, :] = dot(grad_pre, weights[0, r], 1, 1).astype(BF16)
    grad_slots = dot(c1[...], back1[...], 1, 0) * inverse
    for k in range(shards):
        block = grad_slots[k * cap : (k + 1) * cap, :]
        slot_grads[k] = jnp.where(live[k], block, F32(0)).astype(BF16)


def reduce_kernel(
    n_dp,
    n_table,
    seeds,
    slot_grads,
    asked_row,
    grads,
    table_part,
    total_out,
    returned,
    dense,
    dense_send,
    dense_recv,
    inbox,
    running,
    s_slot,
    r_slot,
    s_dp,
    r_dp,
    s_rs,
    r_rs,
    s_ag,
    r_ag,
):
    me = lax.axis_index("table")
    my_dp = lax.axis_index("dp")
    streams, chunks = grads.shape[0], grads.shape[1]
    greet((("table", n_table), ("dp", n_dp)))

    bits = [("table", 1 << b) for b in range(n_table.bit_length() - 1)]
    bits += [("dp", 1 << b) for b in range(n_dp.bit_length() - 1)]
    head, rest = bits[:1], bits[1:]
    orders = []
    for s in range(streams):
        turn = s % max(1, len(rest))
        orders.append(head + rest[turn:] + rest[:turn])
    phases = len(bits)

    def side(axis, bit):
        return lax.rem(lax.axis_index(axis) // bit, 2)

    def partner(axis, bit):
        return peer_on(axis, lax.axis_index(axis) + bit * (1 - 2 * side(axis, bit)))

    def region(p):
        return chunks - (chunks >> p)

    def current(s, p):
        return (grads, 0) if p == 0 else (running, region(p - 1))

    def scatter_copy(s, p):
        axis, bit = orders[s][p]
        half = chunks >> (p + 1)
        ref, start = current(s, p)
        return pltpu.make_async_remote_copy(
            src_ref=ref.at[s, pl.ds(start + (1 - side(axis, bit)) * half, half)],
            dst_ref=inbox.at[s, pl.ds(region(p), half)],
            send_sem=s_rs.at[s, p],
            recv_sem=r_rs.at[s, p],
            device_id=partner(axis, bit),
            device_id_type=MESH,
        )

    def base(s, p):
        place = 0
        for q in range(p):
            axis, bit = orders[s][q]
            place = place + side(axis, bit) * (chunks >> (q + 1))
        return place

    def gather_copy(s, p):
        axis, bit = orders[s][p]
        half = chunks >> (p + 1)
        spot = pl.ds(base(s, p + 1), half)
        return pltpu.make_async_remote_copy(
            src_ref=total_out.at[s, spot],
            dst_ref=total_out.at[s, spot],
            send_sem=s_ag.at[s, p],
            recv_sem=r_ag.at[s, p],
            device_id=partner(axis, bit),
            device_id_type=MESH,
        )

    slot_copies = []
    for step in range(1, n_table):
        peer = lax.rem(me + step, n_table)
        copy = pltpu.make_async_remote_copy(
            src_ref=slot_grads.at[peer],
            dst_ref=returned.at[me],
            send_sem=s_slot.at[step],
            recv_sem=r_slot.at[step],
            device_id=peer_on("table", peer),
            device_id_type=MESH,
        )
        copy.start()
        slot_copies.append(copy)
    scatters = [[scatter_copy(s, 0)] for s in range(streams)]
    for s in range(streams):
        scatters[s][0].start()

    returned[me] = slot_grads[me]
    selector = pick_rows(asked_row[...], dense.shape[0] * dense.shape[1])
    for copy in slot_copies:
        copy.wait()
    rows = returned[...].reshape(selector.shape[1], returned.shape[2])
    dense[...] = dot(selector, rows, 1, 0).reshape(dense.shape)
    dense_send[...] = dense[...].astype(BF16)
    dp_copies = []
    for step in range(1, n_dp):
        peer = lax.rem(my_dp + step, n_dp)
        copy = pltpu.make_async_remote_copy(
            src_ref=dense_send.at[peer],
            dst_ref=dense_recv.at[step],
            send_sem=s_dp.at[step],
            recv_sem=r_dp.at[step],
            device_id=peer_on("dp", peer),
            device_id_type=MESH,
        )
        copy.start()
        dp_copies.append(copy)

    scale = F32(1.0 / math.sqrt(seeds))
    for p in range(phases):
        half = chunks >> (p + 1)
        for s in range(streams):
            axis, bit = orders[s][p]
            scatters[s][p].wait_recv()
            ref, start = current(s, p)
            mine = ref[s, pl.ds(start + side(axis, bit) * half, half)].astype(F32)
            summed = mine + inbox[s, pl.ds(region(p), half)].astype(F32)
            if p < phases - 1:
                running[s, pl.ds(region(p), half)] = summed.astype(BF16)
                copy = scatter_copy(s, p + 1)
                copy.start()
                scatters[s].append(copy)
            else:
                total_out[s, pl.ds(base(s, phases), 1)] = (summed * scale).astype(BF16)
    gathers = []
    for p in reversed(range(phases)):
        for s in range(streams):
            if p < phases - 1:
                gathers[(phases - 2 - p) * streams + s].wait_recv()
            copy = gather_copy(s, p)
            copy.start()
            gathers.append(copy)

    part = dense[my_dp]
    for copy in dp_copies:
        copy.wait()
    for step in range(1, n_dp):
        part = part + dense_recv[step].astype(F32)
    table_part[...] = part

    for s in range(streams):
        gathers[(phases - 1) * streams + s].wait_recv()
        for p in range(phases):
            scatters[s][p].wait_send()
    for copy in gathers:
        copy.wait_send()


def body(
    n_dp,
    n_table,
    table,
    weights,
    fetch_rows,
    fetch_count,
    first_self,
    first_edges,
    first_degree,
    second_self,
    second_edges,
    second_degree,
    cotangent,
):
    wanted = fetch_rows[0, 0]
    shards, cap = wanted.shape
    height, feature = table.shape
    slots = shards * cap
    relations, width1, fan = first_edges.shape[2:]
    width2 = second_edges.shape[3]
    terms = relations + 1
    vmem = pl.BlockSpec(memory_space=VMEM)
    smem = pl.BlockSpec(memory_space=pltpu.SMEM)
    dma = pltpu.SemaphoreType.DMA

    fetched, asked_row = pl.pallas_call(
        functools.partial(fetch_kernel, n_table),
        out_shape=(
            jax.ShapeDtypeStruct((shards, cap, feature), BF16),
            jax.ShapeDtypeStruct((1, slots), jnp.int32),
        ),
        in_specs=[vmem] * 2,
        out_specs=(vmem, vmem),
        scratch_shapes=[
            VMEM((n_table, shards, cap), jnp.int32),
            VMEM((shards, cap, feature), BF16),
            dma((n_table,)),
            dma((n_table,)),
            dma((n_table,)),
            dma((n_table,)),
        ],
        compiler_params=pltpu.CompilerParams(collective_id=0, has_side_effects=True),
    )(table, wanted)

    node_out, grads, slot_grads = pl.pallas_call(
        step_kernel,
        out_shape=(
            jax.ShapeDtypeStruct((width2, feature), BF16),
            jax.ShapeDtypeStruct((2, terms, feature, feature), BF16),
            jax.ShapeDtypeStruct((shards, cap, feature), BF16),
        ),
        in_specs=[smem] + [vmem] * 9,
        out_specs=(vmem,) * 3,
        scratch_shapes=[
            VMEM((slots, terms * width1), BF16),
            VMEM((width1, terms * width2), BF16),
            VMEM((feature, terms * width1), BF16),
            VMEM((feature, terms * width2), BF16),
            VMEM((terms * width1, feature), BF16),
            VMEM((terms * width2, feature), BF16),
        ],
    )(
        fetch_count[0, 0],
        fetched,
        weights,
        first_self[0],
        jnp.swapaxes(first_edges[0, 0], 1, 2),
        first_degree[0, 0][:, None],
        second_self[0],
        jnp.swapaxes(second_edges[0, 0], 1, 2),
        second_degree[0, 0][:, None],
        cotangent[0, 0],
    )

    devices = n_dp * n_table
    total_rows = 2 * terms * feature
    streams = 3 if total_rows % (3 * devices) == 0 else 1
    chunk = total_rows // (streams * devices)
    phases = devices.bit_length() - 1
    pieces = (streams, devices, chunk, feature)
    table_part, total = pl.pallas_call(
        functools.partial(reduce_kernel, n_dp, n_table, width2 * devices),
        out_shape=(
            jax.ShapeDtypeStruct((height // n_dp, feature), F32),
            jax.ShapeDtypeStruct(pieces, BF16),
        ),
        in_specs=[vmem] * 3,
        out_specs=(vmem,) * 2,
        scratch_shapes=[
            VMEM((shards, cap, feature), BF16),
            VMEM((n_dp, height // n_dp, feature), F32),
            VMEM((n_dp, height // n_dp, feature), BF16),
            VMEM((n_dp, height // n_dp, feature), BF16),
            VMEM(pieces, BF16),
            VMEM(pieces, BF16),
            dma((n_table,)),
            dma((n_table,)),
            dma((n_dp,)),
            dma((n_dp,)),
            dma((streams, phases)),
            dma((streams, phases)),
            dma((streams, phases)),
            dma((streams, phases)),
        ],
        compiler_params=pltpu.CompilerParams(collective_id=1, has_side_effects=True),
    )(slot_grads, asked_row, grads.reshape(pieces))
    return (node_out[None, None], total.reshape(weights.shape), table_part[None])


def solution(mesh):
    return jax.shard_map(
        functools.partial(body, mesh.shape["dp"], mesh.shape["table"]),
        mesh=mesh,
        in_specs=(
            P("table", None),
            P(),
            P("dp", "table", None, None),
            P("dp", "table", None),
            P("dp", "table", None),
            P("dp", "table", None, None, None),
            P("dp", "table", None, None),
            P("dp", "table", None),
            P("dp", "table", None, None, None),
            P("dp", "table", None, None),
            P("dp", "table", None, None),
        ),
        out_specs=(P("dp", "table", None, None), P(), P("table", "dp", None)),
        check_vma=False,
    )
```

time: 263 us -> 70.6 us (0.27)
  other arithmetic: 90.3 us -> 0 us
  waiting for transfers between devices: 84.6 us -> 0 us
  Pallas kernels: 0 us -> 66.4 us
  local copies, waits for them, and re-layouts: 44.5 us -> 3.35 us
  between operations: 15.9 us -> 0.66 us
  matrix products: 13 us -> 0 us
  starting transfers between devices: 13 us -> 0 us
    psum x1 -> x0, waiting for transfers between devices: 75.6 us -> none  [body(): grad_bottom, grad_top = lax.psum((grad_bottom, grad_top), ('dp', 'table'))]
    pallas_call x0 -> x3, Pallas kernels: none -> 66.4 us  [the longest x1 47.8 us: body(): pl.pallas_call(functools.partial(reduce_kernel, n_dp, n_table, width2 * d...]
    scatter-add x13 -> x0, other arithmetic: 58.1 us -> none  [the longest x10 51.7 us: spread_single(): running.at[indices.reshape(-1)].add(placed.reshape(-1, part_grad.shape[-1]))]
    gather x23 -> x0, local copies, waits for them, and re-layouts: 34.2 us -> none  [the longest x20 30.4 us: aggregate_single(): features[indices]]
    dot_general x12 -> x0, matrix products: 13 us -> none  [the longest x2 3.97 us: input_terms(): jnp.einsum('be,rde->rbd', grad, layer_weights[1:], preferred_element_type...]
    all_to_all x3 -> x0, starting transfers between devices: 12.9 us -> none  [the longest x1 5.34 us: body(): lax.all_to_all(wanted, 'table', split_axis=0, concat_axis=0, tiled=True)]
    reduce_sum x10 -> x0, other arithmetic: 9.69 us -> none  [aggregate_single(): summed = jnp.sum(picked.astype(jnp.float32), axis=1)]
    all_to_all x3 -> x0, waiting for transfers between devices: 8.98 us -> none  [the longest x1 6.05 us: body(): lax.all_to_all(slot_grads, 'table', split_axis=0, concat_axis=0, tiled=True)]
  transfers between devices with their start and end apart: 5 -> 0, of which waited for: 3 -> 0; matrix products, arithmetic and copies ran while one was open for 32% -> 0% of each run, Pallas kernels for 0% -> 0%
where the time goes in v1:
time: 70.6 us; the launch traced here: 70.4 us
  Pallas kernels  66.4 us (94%)
  local copies, waits for them, and re-layouts  3.35 us (5%)
    pallas_call x1, Pallas kernels, body(): pl.pallas_call(functools.partial(reduce_kernel, n_dp, n_table, width2 * d...  47.8 us
    pallas_call x1, Pallas kernels, body(): pl.pallas_call(functools.partial(fetch_kernel, n_table), out_shape=(jax.S...  12.6 us
    pallas_call x1, Pallas kernels, body(): pl.pallas_call(step_kernel, out_shape=(jax.ShapeDtypeStruct((width2, feat...  5.89 us
    unnamed x4, local copies, waits for them, and re-layouts  3.35 us

profile of v1, /device:TPU:0, one launch (start us, length us, event | category | flops | bytes accessed | tf_op | source)
XLA Modules:
  0.0 70.4 jit_solution(6647666303564155468)
XLA Ops:
  0.6 12.6 %shard_map.130 = (bf16[8,32,256]{2,1,0:T(8,128)(2,1)}, s32[1,256]{1,0:T(1,128)}) custom-call(bf16[512,256]{1,0:T(8,128)(2,1)} %table.1, s32[8,32]{1,0:T(8,128)} %bitcast.24), custom_call_target="tpu_custom_call" | custom-call | tf_op jit(solution)/shard_map/pallas_call | solution.py:363
  13.3 5.9 %shard_map.131 = (bf16[128,256]{1,0:T(8,128)(2,1)}, bf16[2,6,256,256]{3,2,1,0:T(8,128)(2,1)}, bf16[8,32,256]{2,1,0:T(8,128)(2,1)}) custom-call(s32[8]{0:T(128)} %bitcast.27, bf16[8,32,256]{2,1,0:T(8,128)(2,1)} %get-tuple-element.10.fetched, bf16[2,6,256,256]{3,2,1,0:T(8,128)(2,1)} %weights.1, s32[1,256]{1,0:T(1,128)} %bitcast.26, s32[5,4,256]{2,1,0:T(4,128)} %bitcast.21, ...), custom_call_target="tpu_custom_call" | custom-call | tf_op jit(solution)/shard_map/pallas_call | solution.py:382
  19.1 47.8 %shard_map.132 = (f32[128,256]{1,0:T(8,128)}, bf16[3,32,32,256]{3,2,1,0:T(8,128)(2,1)}) custom-call(bf16[8,32,256]{2,1,0:T(8,128)(2,1)} %get-tuple-element.12.slot_grads, s32[1,256]{1,0:T(1,128)} %get-tuple-element.13.asked_row, bf16[3,32,32,256]{3,2,1,0:T(8,128)(2,1)} %bitcast.17), custom_call_target="tpu_custom_call" | custom-call | tf_op jit(solution)/shard_map/pallas_call | solution.py:418
  67.0 0.0 copy-start
  67.0 2.7 %copy.16 = bf16[2,6,256,256]{3,2,1,0:T(8,128)(2,1)} copy(bf16[2,6,256,256]{3,2,1,0:T(8,128)(2,1)} %bitcast.18) | data formatting | bytes 3145728
  69.7 0.0 copy-done
  69.7 0.7 copy.17
Async XLA Ops:
  67.0 2.7 %copy-start = (f32[128,256]{1,0:T(8,128)S(1)}, f32[128,256]{1,0:T(8,128)}, u32[]{:S(2)}) copy-start(f32[128,256]{1,0:T(8,128)} %get-tuple-element.16) | copy-start | bytes 393220

commit v2 on v1

v2 whole, which is shorter than its diff:
```python
import functools
import math

import jax
import jax.numpy as jnp
from jax import lax
from jax.experimental import pallas as pl
from jax.experimental.pallas import tpu as pltpu
from jax.sharding import PartitionSpec as P

MESH = pl.DeviceIdType.MESH
VMEM = pltpu.VMEM
F32 = jnp.float32
BF16 = jnp.bfloat16


def dot(a, b, da, db):
    return lax.dot_general(a, b, (((da,), (db,)), ((), ())), preferred_element_type=F32)


def peer_on(axis, index):
    if axis == "dp":
        return (index, lax.axis_index("table"))
    return (lax.axis_index("dp"), index)


def greet(axes_sizes):
    barrier = pltpu.get_barrier_semaphore()
    total = 0
    for axis, size in axes_sizes:
        me = lax.axis_index(axis)
        for step in range(1, size):
            pl.semaphore_signal(
                barrier,
                inc=1,
                device_id=peer_on(axis, lax.rem(me + step, size)),
                device_id_type=MESH,
            )
            total += 1
    return lambda: pl.semaphore_wait(barrier, total)


def pick_rows(row_numbers, height):
    shape = (height, row_numbers.shape[1])
    match = lax.broadcasted_iota(jnp.int32, shape, 0) == row_numbers
    return jnp.where(match, F32(1), F32(0)).astype(BF16)


def fetch_kernel(
    n_table, table, wanted, fetched, asked_row, asked_all, found, ssem, rsem, ssem2, rsem2
):
    me = lax.axis_index("table")
    greet((("table", n_table),))()
    sends = []
    for step in range(1, n_table):
        copy = pltpu.make_async_remote_copy(
            src_ref=wanted,
            dst_ref=asked_all.at[me],
            send_sem=ssem.at[step],
            recv_sem=rsem.at[step],
            device_id=peer_on("table", lax.rem(me + step, n_table)),
            device_id_type=MESH,
        )
        copy.start()
        sends.append(copy)
    asked_all[me] = wanted[...]
    for copy in sends:
        copy.wait_recv()
    row = jnp.concatenate([asked_all[j, pl.ds(me, 1), :] for j in range(n_table)], axis=1)
    asked_row[...] = row
    selector = pick_rows(row, table.shape[0])
    found[...] = dot(selector, table[...], 0, 0).astype(BF16).reshape(found.shape)
    replies = []
    for step in range(1, n_table):
        peer = lax.rem(me + step, n_table)
        copy = pltpu.make_async_remote_copy(
            src_ref=found.at[peer],
            dst_ref=fetched.at[me],
            send_sem=ssem2.at[step],
            recv_sem=rsem2.at[step],
            device_id=peer_on("table", peer),
            device_id_type=MESH,
        )
        copy.start()
        replies.append(copy)
    fetched[me] = found[me]
    for copy in sends:
        copy.wait_send()
    for copy in replies:
        copy.wait()


def step_kernel(
    n_dp,
    n_table,
    seeds,
    counts,
    fetched,
    asked_row,
    weights,
    self1,
    edges1,
    degree1,
    self2,
    edges2,
    degree2,
    cot,
    node_out,
    table_part,
    total_out,
    c1,
    c2,
    x1t,
    x2t,
    back1,
    back2,
    slot_grads,
    grads,
    returned,
    dense,
    dense_send,
    dense_recv,
    inbox,
    running,
    outgoing,
    s_slot,
    r_slot,
    s_dp,
    r_dp,
    s_rs,
    r_rs,
    s_ag,
    r_ag,
):
    entered = greet((("table", n_table), ("dp", n_dp)))
    relations, fan, width1 = edges1.shape
    width2 = edges2.shape[2]
    shards, cap, feature = fetched.shape
    slots = shards * cap
    terms = relations + 1
    common = math.lcm(*range(1, fan + 1))
    inverse = F32(1.0 / common)
    me = lax.axis_index("table")
    my_dp = lax.axis_index("dp")
    streams, chunks, chunk = grads.shape[:3]

    pair = n_table // max(1, n_table // 2)
    across = n_table // pair
    mine_pair, mine_across = lax.rem(me, pair), me // pair
    twin = (pair, mine_pair, lambda j: peer_on("table", mine_across * pair + j))
    plane = (across, mine_across, lambda j: peer_on("table", j * pair + mine_pair))
    column = (n_dp, my_dp, lambda j: peer_on("dp", j))
    orders = [(twin, column, plane) if s == 1 else (twin, plane, column) for s in range(streams)]

    def held(s, p):
        left = chunks
        for group in orders[s][:p]:
            left //= group[0]
        return left

    def region(s, p):
        return sum(held(s, q) for q in range(1, p))

    def slot(s, p, step):
        before = sum((orders[s][q][0] - 1) * held(s, q + 1) for q in range(p))
        return before + (step - 1) * held(s, p + 1)

    def base(s, p):
        place = 0
        for q in range(p):
            place = place + orders[s][q][1] * held(s, q + 1)
        return place

    started = {}

    def scatter(s, p):
        size, place, device = orders[s][p]
        part = held(s, p + 1)
        source, start = (grads, 0) if p == 0 else (outgoing, region(s, p))
        copies = []
        for step in range(1, size):
            to = lax.rem(place + step, size)
            copy = pltpu.make_async_remote_copy(
                src_ref=source.at[s, pl.ds(start + to * part, part)],
                dst_ref=inbox.at[s, pl.ds(slot(s, p, step), part)],
                send_sem=s_rs.at[s, p, step],
                recv_sem=r_rs.at[s, p, step],
                device_id=device(to),
                device_id_type=MESH,
            )
            copy.start()
            copies.append(copy)
        started["rs", s, p] = copies

    def absorb(s, p):
        size, place, device = orders[s][p]
        part = held(s, p + 1)
        source, start = (grads, 0) if p == 0 else (running, region(s, p))
        where = pl.ds(region(s, p + 1), part)
        summed = source[s, pl.ds(start + place * part, part)].astype(F32)
        for step in range(1, size):
            started["rs", s, p][step - 1].wait_recv()
            summed = summed + inbox[s, pl.ds(slot(s, p, step), part)].astype(F32)
        if p < len(orders[s]) - 1:
            running[s, where] = summed
            outgoing[s, where] = summed.astype(BF16)
            scatter(s, p + 1)
        else:
            scale = F32(1.0 / math.sqrt(seeds))
            total_out[s, pl.ds(base(s, p + 1), part)] = (summed * scale).astype(BF16)

    def gather(s, p):
        size, place, device = orders[s][p]
        spot = pl.ds(base(s, p + 1), held(s, p + 1))
        copies = []
        for step in range(1, size):
            copy = pltpu.make_async_remote_copy(
                src_ref=total_out.at[s, spot],
                dst_ref=total_out.at[s, spot],
                send_sem=s_ag.at[s, p, step],
                recv_sem=r_ag.at[s, p, step],
                device_id=device(lax.rem(place + step, size)),
                device_id_type=MESH,
            )
            copy.start()
            copies.append(copy)
        started["ag", s, p] = copies

    def keep(block, value):
        first = block * feature // chunk
        for c in range(feature // chunk):
            s, at = divmod(first + c, chunks)
            grads[s, at] = value[c * chunk : (c + 1) * chunk, :].astype(BF16)

    live = []
    slot_pos = lax.broadcasted_iota(jnp.int32, (cap, feature), 0)
    for k in range(shards):
        live.append(slot_pos < counts[k])
    inputs = jnp.concatenate(
        [jnp.where(live[k], fetched[k].astype(F32), F32(0)) for k in range(shards)], axis=0
    ).astype(BF16)

    def fill(selector, own, edges, degree, height, width):
        spot = lax.broadcasted_iota(jnp.int32, (height, width), 0)
        selector[:, :width] = jnp.where(spot == own[...], F32(common), F32(0)).astype(BF16)
        for r in range(relations):
            deg = degree[r]
            share = jnp.zeros(deg.shape, F32)
            for d in range(1, fan + 1):
                share = jnp.where(deg == d, F32(common // d), share)
            total = jnp.zeros((height, width), F32)
            for f in range(fan):
                where = jnp.where(deg > f, edges[r, f : f + 1, :], -1)
                total = total + jnp.where(spot == where, share, F32(0))
            selector[:, (r + 1) * width : (r + 2) * width] = total.astype(BF16)

    fill(c1, self1, edges1, degree1, slots, width1)
    fill(c2, self2, edges2, degree2, width1, width2)

    x1t[...] = (dot(inputs, c1[...], 0, 0) * inverse).astype(BF16)
    pre = jnp.zeros((width1, feature), F32)
    for r in range(terms):
        pre = pre + dot(x1t[:, r * width1 : (r + 1) * width1], weights[0, r], 0, 0)
    s = 1.0 / (1.0 + jnp.exp(-pre))
    hidden = (pre * s).astype(BF16)
    slope = s * (1.0 + pre * (1.0 - s))

    x2t[...] = (dot(hidden, c2[...], 0, 0) * inverse).astype(BF16)
    cot_rows = cot[...]
    for r in range(terms):
        part = x2t[:, r * width2 : (r + 1) * width2]
        keep(terms + r, dot(part, cot_rows, 1, 0))
    early = [n for n in range(streams) if n * chunks * chunk >= terms * feature]
    late = [n for n in reversed(range(streams)) if n not in early]
    entered()
    for n in early:
        scatter(n, 0)

    for r in range(terms):
        back2[r * width2 : (r + 1) * width2, :] = dot(cot_rows, weights[1, r], 1, 1).astype(BF16)
    grad_hidden = dot(c2[...], back2[...], 1, 0) * inverse
    grad_pre = (grad_hidden * slope).astype(BF16)
    for r in range(terms):
        part = x1t[:, r * width1 : (r + 1) * width1]
        keep(r, dot(part, grad_pre, 1, 0))
    for n in late:
        scatter(n, 0)
    for n in early:
        absorb(n, 0)

    for r in range(terms):
        back1[r * width1 : (r + 1) * width1, :] = dot(grad_pre, weights[0, r], 1, 1).astype(BF16)
    grad_slots = dot(c1[...], back1[...], 1, 0) * inverse
    for k in range(shards):
        block = grad_slots[k * cap : (k + 1) * cap, :]
        slot_grads[k] = jnp.where(live[k], block, F32(0)).astype(BF16)
    slot_copies = []
    for step in range(1, n_table):
        peer = lax.rem(me + step, n_table)
        copy = pltpu.make_async_remote_copy(
            src_ref=slot_grads.at[peer],
            dst_ref=returned.at[me],
            send_sem=s_slot.at[step],
            recv_sem=r_slot.at[step],
            device_id=peer_on("table", peer),
            device_id_type=MESH,
        )
        copy.start()
        slot_copies.append(copy)
    returned[me] = slot_grads[me]
    for n in late:
        absorb(n, 0)

    out = jnp.zeros((width2, feature), F32)
    for r in range(terms):
        out = out + dot(x2t[:, r * width2 : (r + 1) * width2], weights[1, r], 0, 0)
    node_out[...] = out.astype(BF16)
    selector = pick_rows(asked_row[...], dense.shape[0] * dense.shape[1])
    for copy in slot_copies:
        copy.wait()
    rows = returned[...].reshape(selector.shape[1], feature)
    dense[...] = dot(selector, rows, 1, 0).reshape(dense.shape)
    dense_send[...] = dense[...].astype(BF16)
    dp_copies = []
    for step in range(1, n_dp):
        peer = lax.rem(my_dp + step, n_dp)
        copy = pltpu.make_async_remote_copy(
            src_ref=dense_send.at[peer],
            dst_ref=dense_recv.at[step],
            send_sem=s_dp.at[step],
            recv_sem=r_dp.at[step],
            device_id=peer_on("dp", peer),
            device_id_type=MESH,
        )
        copy.start()
        dp_copies.append(copy)

    turn = early + late
    for n in turn:
        absorb(n, 1)
    for n in turn:
        absorb(n, 2)
        gather(n, 2)
    shard = dense[my_dp]
    for copy in dp_copies:
        copy.wait()
    for step in range(1, n_dp):
        shard = shard + dense_recv[step].astype(F32)
    table_part[...] = shard
    for p in (1, 0):
        for n in turn:
            for copy in started["ag", n, p + 1]:
                copy.wait_recv()
            gather(n, p)
    for n in turn:
        for copy in started["ag", n, 0]:
            copy.wait_recv()
        for p in range(3):
            for copy in started["rs", n, p] + started["ag", n, p]:
                copy.wait_send()


def body(
    n_dp,
    n_table,
    table,
    weights,
    fetch_rows,
    fetch_count,
    first_self,
    first_edges,
    first_degree,
    second_self,
    second_edges,
    second_degree,
    cotangent,
):
    wanted = fetch_rows[0, 0]
    shards, cap = wanted.shape
    height, feature = table.shape
    slots = shards * cap
    relations, width1, fan = first_edges.shape[2:]
    width2 = second_edges.shape[3]
    terms = relations + 1
    vmem = pl.BlockSpec(memory_space=VMEM)
    smem = pl.BlockSpec(memory_space=pltpu.SMEM)
    dma = pltpu.SemaphoreType.DMA

    fetched, asked_row = pl.pallas_call(
        functools.partial(fetch_kernel, n_table),
        out_shape=(
            jax.ShapeDtypeStruct((shards, cap, feature), BF16),
            jax.ShapeDtypeStruct((1, slots), jnp.int32),
        ),
        in_specs=[vmem] * 2,
        out_specs=(vmem, vmem),
        scratch_shapes=[
            VMEM((n_table, shards, cap), jnp.int32),
            VMEM((shards, cap, feature), BF16),
            dma((n_table,)),
            dma((n_table,)),
            dma((n_table,)),
            dma((n_table,)),
        ],
        compiler_params=pltpu.CompilerParams(collective_id=0, has_side_effects=True),
    )(table, wanted)

    devices = n_dp * n_table
    total_rows = 2 * terms * feature
    streams = 3 if total_rows % (3 * devices) == 0 else 1
    chunk = total_rows // (streams * devices)
    pieces = (streams, devices, chunk, feature)
    widest = max(2, n_table // 2, n_dp)
    ways = (streams, 3, widest)
    node_out, table_part, total = pl.pallas_call(
        functools.partial(step_kernel, n_dp, n_table, width2 * devices),
        out_shape=(
            jax.ShapeDtypeStruct((width2, feature), BF16),
            jax.ShapeDtypeStruct((height // n_dp, feature), F32),
            jax.ShapeDtypeStruct(pieces, BF16),
        ),
        in_specs=[smem] + [vmem] * 10,
        out_specs=(vmem,) * 3,
        scratch_shapes=[
            VMEM((slots, terms * width1), BF16),
            VMEM((width1, terms * width2), BF16),
            VMEM((feature, terms * width1), BF16),
            VMEM((feature, terms * width2), BF16),
            VMEM((terms * width1, feature), BF16),
            VMEM((terms * width2, feature), BF16),
            VMEM((shards, cap, feature), BF16),
            VMEM(pieces, BF16),
            VMEM((shards, cap, feature), BF16),
            VMEM((n_dp, height // n_dp, feature), F32),
            VMEM((n_dp, height // n_dp, feature), BF16),
            VMEM((n_dp, height // n_dp, feature), BF16),
            VMEM(pieces, BF16),
            VMEM(pieces, F32),
            VMEM(pieces, BF16),
            dma((n_table,)),
            dma((n_table,)),
            dma((n_dp,)),
            dma((n_dp,)),
            dma(ways),
            dma(ways),
            dma(ways),
            dma(ways),
        ],
        compiler_params=pltpu.CompilerParams(collective_id=1, has_side_effects=True),
    )(
        fetch_count[0, 0],
        fetched,
        asked_row,
        weights,
        first_self[0],
        jnp.swapaxes(first_edges[0, 0], 1, 2),
        first_degree[0, 0][:, None],
        second_self[0],
        jnp.swapaxes(second_edges[0, 0], 1, 2),
        second_degree[0, 0][:, None],
        cotangent[0, 0],
    )
    return (node_out[None, None], total.reshape(weights.shape), table_part[None])


def solution(mesh):
    return jax.shard_map(
        functools.partial(body, mesh.shape["dp"], mesh.shape["table"]),
        mesh=mesh,
        in_specs=(
            P("table", None),
            P(),
            P("dp", "table", None, None),
            P("dp", "table", None),
            P("dp", "table", None),
            P("dp", "table", None, None, None),
            P("dp", "table", None, None),
            P("dp", "table", None),
            P("dp", "table", None, None, None),
            P("dp", "table", None, None),
            P("dp", "table", None, None),
        ),
        out_specs=(P("dp", "table", None, None), P(), P("table", "dp", None)),
        check_vma=False,
    )
```

time: 70.6 us -> 56 us (0.79)
  Pallas kernels: 66.4 us -> 50.3 us
  local copies, waits for them, and re-layouts: 3.35 us -> 4.82 us
    pallas_call x2 -> x1, Pallas kernels: 53.7 us -> 37.6 us  [body(): pl.pallas_call(functools.partial(step_kernel, n_dp, n_table, width2 * dev...]
    unnamed x4 -> x5, local copies, waits for them, and re-layouts: 3.35 us -> 4.82 us
where the time goes in v2:
time: 56 us; the launch traced here: 55.7 us
  Pallas kernels  50.3 us (90%)
  local copies, waits for them, and re-layouts  4.82 us (9%)
  between operations  0.65 us (1%)
    pallas_call x1, Pallas kernels, body(): pl.pallas_call(functools.partial(step_kernel, n_dp, n_table, width2 * dev...  37.6 us
    pallas_call x1, Pallas kernels, body(): pl.pallas_call(functools.partial(fetch_kernel, n_table), out_shape=(jax.S...  12.6 us
    unnamed x5, local copies, waits for them, and re-layouts  4.82 us

profile of v2, /device:TPU:0, one launch (start us, length us, event | category | flops | bytes accessed | tf_op | source)
XLA Modules:
  0.0 55.7 jit_solution(12722172808205609021)
XLA Ops:
  0.6 12.6 %shard_map.130 = (bf16[8,32,256]{2,1,0:T(8,128)(2,1)}, s32[1,256]{1,0:T(1,128)}) custom-call(bf16[512,256]{1,0:T(8,128)(2,1)} %table.1, s32[8,32]{1,0:T(8,128)} %bitcast.23), custom_call_target="tpu_custom_call" | custom-call | tf_op jit(solution)/shard_map/pallas_call | solution.py:389
  13.3 37.6 %shard_map.131 = (bf16[128,256]{1,0:T(8,128)(2,1)}, f32[128,256]{1,0:T(8,128)}, bf16[3,32,32,256]{3,2,1,0:T(8,128)(2,1)}) custom-call(s32[8]{0:T(128)} %bitcast.26, bf16[8,32,256]{2,1,0:T(8,128)(2,1)} %get-tuple-element.8.fetched, s32[1,256]{1,0:T(1,128)} %get-tuple-element.9.asked_row, bf16[2,6,256,256]{3,2,1,0:T(8,128)(2,1)} %weights.1, ...), custom_call_target="tpu_custom_call" | custom-call | tf_op jit(solution)/shard_map/pallas_call | solution.py:415
  50.9 1.5 %copy.17 = bf16[1,1,128,256]{3,2,1,0:T(8,128)(2,1)} copy(bf16[1,1,128,256]{3,2,1,0:T(8,128)(2,1)} %bitcast.19) | data formatting | bytes 131072
  52.4 0.0 copy-start
  52.4 2.7 %copy.18 = bf16[2,6,256,256]{3,2,1,0:T(8,128)(2,1)} copy(bf16[2,6,256,256]{3,2,1,0:T(8,128)(2,1)} %bitcast.16) | data formatting | bytes 3145728
  55.1 0.0 copy-done
  55.1 0.7 %copy.19 = f32[1,128,256]{2,1,0:T(8,128)} copy(f32[1,128,256]{2,1,0:T(8,128)S(1)} %bitcast.17) | data formatting | bytes 262144
Async XLA Ops:
  52.4 2.7 %copy-start = (f32[128,256]{1,0:T(8,128)S(1)}, f32[128,256]{1,0:T(8,128)}, u32[]{:S(2)}) copy-start(f32[128,256]{1,0:T(8,128)} %get-tuple-element.12) | copy-start | bytes 393220
